TPU v7x, 256 devices: a whole 4x4x8 slice. The times are simulated.
256 devices in a mesh: nodes: 128 (over y, z, x), feat: 2 (over core).
Axes of the slice: x: 4, y: 4, z: 8, core: 2. Of those that a mesh axis runs over, the one named last changes fastest.
Arguments:
- features: bfloat16 [65536, 128], P('nodes'), may hold values from -6 to 6
- row_counts: int32 [128], P('nodes'), may hold values from 128 to 512, as said below
- send_rows: int32 [128, 128, 64], P('nodes'), may hold values from 0 to 511, as said below
- edge_src: int32 [2, 524288], P(None, 'nodes'), may hold values from 0 to 8703, as said below
- edge_dst: int32 [2, 524288], P(None, 'nodes'), may hold values from 0 to 511, as said below
- edge_keep: int32 [2, 524288], P(None, 'nodes'), may hold values 0 or 1
- w_first: bfloat16 [128, 512], P(None, 'feat'), may hold values from -0.5 to 0.5
- b_first: float32 [512], P('feat'), may hold values from -3 to 3
- w_second: bfloat16 [512, 512], P(None, 'feat'), may hold values from -0.25 to 0.25
Outputs:
- normed: bfloat16 [2, 65536, 512], P(None, 'nodes', 'feat')
- correlation: float32 [512, 512], P('nodes', 'feat')
- barlow_loss: float32 [], replicated
Inputs may be any that keep to these rules, and one draw needn't show every extreme that they name: `row_counts`: some partition has all 512 rows live. send_rows[i, j, h] is below row_counts[i]. `edge_src`: A source below 512 is below row_counts of the edge's partition. `edge_dst`: A partition's edge slots come in aligned blocks of 1024 slots; block k targets rows k * 128 to (k + 1) * 128 - 1.
All inputs are finite; a program needn't handle non-finite values. No bound on the sum of `edge_keep` on one device may be relied on, other than what follows from the above.
Results may differ from a plain program's by a relative error of at most 0.0017.
The roundings to bfloat16 on the way count: a program that leaves them out, or rounds other values in their place, can miss the bound.
Values may be sent and summed in bfloat16 or wider, within the bound.
No kernel may reach another device: no remote copies, remote signals or barrier semaphores. Data moves between devices by JAX's collectives and lax.ppermute only.
A program may use at most 64 MiB of HBM per device.

v0:
```python
import jax
import jax.numpy as jnp
from jax import lax
from jax.sharding import Mesh
from jax.sharding import PartitionSpec as P

NODES = ("nodes_0", "nodes_1", "nodes_2")
NODES_FEAT = ("nodes_0", "nodes_1", "nodes_2", "feat")


def joined_along(tiles, dim):
    shape = list(tiles.shape[1:])
    shape[dim] *= tiles.shape[0]
    return jnp.moveaxis(tiles, 0, dim).reshape(shape)


def from_everyone(shard, axis):
    devices = lax.axis_size(axis)
    return lax.all_to_all(
        jnp.broadcast_to(shard[None], (devices, *shard.shape)), axis, 0, 0, tiled=True
    )


def gathered_copies(shard, axis, dim):
    return joined_along(from_everyone(shard, axis), dim)


def over_axes(shard, axes):
    for axis in axes:
        shard = lax.psum(shard, axis)
    return shard


def own_rows(running, axes):
    for axis in axes:
        running = lax.psum_scatter(running, axis, scatter_dimension=0, tiled=True)
    return running


def per_device(
    features, row_counts, send_rows, edge_src, edge_dst, edge_keep, w_first, b_first, w_second
):
    local_rows = features.shape[0]
    partitions = lax.axis_size(NODES)
    halo_rows = send_rows.shape[2]
    edge_total = edge_src.shape[1]
    tile_rows = min(128, local_rows)
    tiles = local_rows // tile_rows
    per_tile = edge_total // tiles
    live_rows = (jnp.arange(local_rows) < row_counts[0]).astype(jnp.float32)[:, None]
    kept_edges = edge_keep.astype(jnp.float32)
    outbound = send_rows[0]
    tile_base = (jnp.arange(tiles, dtype=jnp.int32) * tile_rows)[:, None]
    row_slots = jnp.arange(tile_rows, dtype=jnp.int32)
    tables = []
    degrees = []
    for view_index in range(2):
        inside = edge_dst[view_index].reshape(tiles, per_tile) - tile_base
        table = (inside[:, :, None] == row_slots[None, None, :]).astype(jnp.float32) * kept_edges[
            view_index
        ].reshape(tiles, per_tile)[:, :, None]
        tables.append(table)
        degrees.append(jnp.sum(table, 1).reshape(local_rows))

    def mix_view(lookup, view_index):
        width = lookup.shape[1]
        picked = lookup[edge_src[view_index]].astype(jnp.float32).reshape(tiles, per_tile, width)
        summed = jnp.einsum(
            "tes,tec->tsc",
            tables[view_index],
            picked,
            precision=lax.Precision.HIGHEST,
            preferred_element_type=jnp.float32,
        )
        summed = summed.reshape(local_rows, width)
        return (lookup[:local_rows].astype(jnp.float32) + summed) / (1.0 + degrees[view_index])[
            :, None
        ]

    arrived = lax.all_to_all(features[outbound], NODES, split_axis=0, concat_axis=0, tiled=True)
    lookup = jnp.concatenate([features, arrived.reshape(partitions * halo_rows, -1)], 0)
    weights_wide = w_first.astype(jnp.float32)
    averaged = [
        jnp.dot(mix_view(lookup, view_index), weights_wide, precision=lax.Precision.HIGHEST)
        for view_index in range(2)
    ]
    hidden = jnp.stack([jax.nn.relu(branch + b_first) for branch in averaged]).astype(jnp.bfloat16)
    summed_second = jnp.einsum(
        "gnq,qm->gnm",
        gathered_copies(hidden, "feat", 2),
        w_second,
        preferred_element_type=jnp.float32,
    )
    projected = summed_second.astype(jnp.bfloat16)
    arrived_second = lax.all_to_all(
        projected[:, outbound], NODES, split_axis=1, concat_axis=1, tiled=True
    )
    embedded = jnp.stack(
        [
            mix_view(
                jnp.concatenate(
                    [
                        projected[view_index],
                        arrived_second[view_index].reshape(partitions * halo_rows, -1),
                    ],
                    0,
                ),
                view_index,
            )
            for view_index in range(2)
        ]
    )
    column_sums, squares, node_total = (
        over_axes(jnp.sum(embedded * live_rows, 1), NODES),
        over_axes(jnp.sum(jnp.square(embedded) * live_rows, 1), NODES),
        over_axes(row_counts[0].astype(jnp.float32), NODES),
    )
    average = column_sums / node_total
    variance = squares / node_total - jnp.square(average)
    normed = (
        (embedded - average[:, None, :]) / jnp.sqrt(variance + 1e-05)[:, None, :] * live_rows
    ).astype(jnp.bfloat16)
    wide_first = gathered_copies(normed[0], "feat", 1)
    row_share = wide_first.shape[1] // partitions
    contract_rows = (((0,), (0,)), ((), ()))
    owned_rows = own_rows(
        lax.dot_general(wide_first, normed[1], contract_rows, preferred_element_type=jnp.float32),
        NODES,
    )
    correlation = owned_rows / node_total
    own_columns = correlation.shape[1]
    row_labels = lax.axis_index(NODES) * row_share + jnp.arange(row_share, dtype=jnp.int32)[:, None]
    column_labels = (
        lax.axis_index("feat") * own_columns + jnp.arange(own_columns, dtype=jnp.int32)[None, :]
    )
    partial_loss = jnp.sum(
        jnp.where(
            row_labels == column_labels,
            jnp.square(1.0 - correlation),
            0.005 * jnp.square(correlation),
        )
    )
    barlow_loss = over_axes(partial_loss, NODES_FEAT)
    return (normed, correlation, barlow_loss)


def solution(mesh):
    torus = Mesh(
        mesh.devices.reshape(4, 8, 4, mesh.shape["feat"]), ("nodes_0", "nodes_1", "nodes_2", "feat")
    )
    placed = (
        P(NODES, None),
        P(NODES),
        P(NODES, None, None),
        P(None, NODES),
        P(None, NODES),
        P(None, NODES),
        P(None, "feat"),
        P("feat"),
        P(None, "feat"),
    )
    return jax.shard_map(
        per_device,
        mesh=torus,
        in_specs=placed,
        out_specs=(P(None, NODES, "feat"), P(NODES, "feat"), P()),
        check_vma=False,
    )
```

profile of v0, /device:TPU:1, one launch (start us, length us, event | category | flops | bytes accessed | tf_op | source)
XLA Modules:
  0.0 631.1 jit_solution(14449898697765373779)
XLA Ops:
  7.2 0.0 copy-start
  7.2 0.8 compare_select_fusion.2
  8.0 0.1 copy.19
  8.1 0.1 reshape.249
  8.2 0.0 copy-done.2
  8.2 29.2 %gather_fusion = bf16[8192,128]{1,0:T(8,128)(2,1)} fusion(bf16[512,128]{1,0:T(8,128)(2,1)S(1)} %copy-done.2, s32[8192]{0:T(1024)S(1)} %broadcast_clamp_fusion), kind=kCustom, calls=%fused_computation | custom fusion | bytes 4227072 | tf_op jit(solution)/shard_map/gather | solution.py:80
  37.5 16.5 %all-to-all-start = ((bf16[128,64,128]{2,1,0:T(8,128)(2,1)}), bf16[128,64,128]{2,1,0:T(8,128)(2,1)S(1)}, u32[]{:S(2)}, u32[]{:S(2)}) async-start(bf16[128,64,128]{2,1,0:T(8,128)(2,1)} %bitcast.1), calls=%async_computation | async-start | bytes 4194304 | tf_op jit(solution)/shard_map/all_to_all | solution.py:80
  53.9 0.1 slice_reduce_fusion.3
  54.1 0.1 slice_reduce_fusion.1
  54.2 0.1 broadcast_subtract_fusion.1
  54.3 0.5 select_reduce_fusion
  55.0 48.3 %all-to-all-done = bf16[128,64,128]{2,1,0:T(8,128)(2,1)S(1)} async-done(((bf16[128,64,128]{2,1,0:T(8,128)(2,1)}), bf16[128,64,128]{2,1,0:T(8,128)(2,1)S(1)}, u32[]{:S(2)}, u32[]{:S(2)}) %all-to-all-start) | async-done | bytes 2097184 | tf_op jit(solution)/shard_map/all_to_all | solution.py:80
  103.3 1.3 copy-done.3
  104.6 1.8 pad_maximum_fusion.2
  106.5 14.9 %gather_fusion.1 = bf16[4096,128]{1,0:T(8,128)(2,1)} fusion(bf16[8704,128]{1,0:T(8,128)(2,1)S(1)} %pad_maximum_fusion.2, s32[4096]{0:T(1024)S(1)} %broadcast_clamp_fusion.2), kind=kCustom, calls=%fused_computation.1 | custom fusion | bytes 2113536 | tf_op jit(solution)/shard_map/gather | solution.py:67
  121.4 2.5 fusion.6
  123.9 14.9 %gather_fusion.2 = bf16[4096,128]{1,0:T(8,128)(2,1)} fusion(bf16[8704,128]{1,0:T(8,128)(2,1)S(1)} %pad_maximum_fusion.2, s32[4096]{0:T(1024)S(1)} %broadcast_clamp_fusion.1), kind=kCustom, calls=%fused_computation.2 | custom fusion | bytes 2113536 | tf_op jit(solution)/shard_map/gather | solution.py:67
  138.8 2.5 fusion.2
  141.3 0.4 fusion.13
  141.7 0.4 fusion.12
  142.2 0.1 pad_maximum_fusion.4
  142.2 0.1 broadcast_in_dim.6
  142.3 8.2 %all_to_all.20 = bf16[2,2,512,256]{3,2,1,0:T(8,128)(2,1)S(1)} all-to-all(bf16[2,2,512,256]{3,2,1,0:T(8,128)(2,1)S(1)} %broadcast_in_dim.6), channel_id=1, replica_groups=mesh['nodes_0'=4,'nodes_1'=8,'nodes_2'=4,'feat'=2] {'feat'}, dimensions={0} | all-to-all | bytes 2097152 | tf_op jit(solution)/shard_map/all_to_all | solution.py:19
  150.5 0.1 copy.28
  150.6 0.4 convolution_convert_fusion
  151.0 0.5 copy.21
  151.6 63.9 %gather_fusion.3 = bf16[8192,2,256]{2,1,0:T(2,128)(2,1)} fusion(bf16[2,512,256]{2,0,1:T(2,128)(2,1)S(1)} %copy.21, s32[8192]{0:T(1024)S(1)} %broadcast_clamp_fusion), kind=kCustom, calls=%fused_computation.3 | custom fusion | bytes 16809984 | tf_op jit(solution)/shard_map/gather | solution.py:96
  215.5 8.6 %copy.30 = bf16[128,64,2,256]{3,1,2,0:T(8,128)(2,1)} copy(bf16[128,64,2,256]{3,2,1,0:T(2,128)(2,1)} %bitcast.76) | data formatting | bytes 16777216 | tf_op jit(solution)/shard_map/gather | solution.py:96
  224.0 7.7 %all-to-all-start.2 = ((bf16[2,128,64,256]{3,2,0,1:T(8,128)(2,1)}), bf16[2,128,64,256]{3,2,0,1:T(8,128)(2,1)}, u32[]{:S(2)}, u32[]{:S(2)}) async-start(bf16[2,128,64,256]{3,2,0,1:T(8,128)(2,1)} %bitcast.75), calls=%async_computation.2 | async-start | bytes 16777216 | tf_op jit(solution)/shard_map/all_to_all | solution.py:95
  231.7 0.0 reduce-scatter.3.cloned.1.call-start
  232.4 180.0 %all-to-all-done.2 = bf16[2,128,64,256]{3,2,0,1:T(8,128)(2,1)} async-done(((bf16[2,128,64,256]{3,2,0,1:T(8,128)(2,1)}), bf16[2,128,64,256]{3,2,0,1:T(8,128)(2,1)}, u32[]{:S(2)}, u32[]{:S(2)}) %all-to-all-start.2) | async-done | bytes 8388640 | tf_op jit(solution)/shard_map/all_to_all | solution.py:95
  412.5 5.3 fusion.41
  417.8 2.8 pad_maximum_fusion.1
  420.6 15.8 %gather_fusion.5 = bf16[4096,256]{1,0:T(8,128)(2,1)S(1)} fusion(bf16[8704,256]{1,0:T(8,128)(2,1)} %pad_maximum_fusion.1, s32[4096]{0:T(1024)S(1)} %broadcast_clamp_fusion.1), kind=kCustom, calls=%fused_computation.5 | custom fusion | bytes 4210688 | tf_op jit(solution)/shard_map/gather | solution.py:67
  436.5 2.1 fusion
  438.5 4.0 pad_maximum_fusion
  442.6 15.8 %gather_fusion.4 = bf16[4096,256]{1,0:T(8,128)(2,1)S(1)} fusion(bf16[8704,256]{1,0:T(8,128)(2,1)} %pad_maximum_fusion, s32[4096]{0:T(1024)S(1)} %broadcast_clamp_fusion.2), kind=kCustom, calls=%fused_computation.4 | custom fusion | bytes 4210688 | tf_op jit(solution)/shard_map/gather | solution.py:67
  458.4 0.0 copy-start.5
  458.4 1.3 fusion.4
  459.7 0.2 fusion.27
  459.9 0.2 multiply_reduce_fusion
  460.2 8.5 %all-reduce.3 = (f32[2,256]{1,0:T(2,128)S(1)}, f32[]{:T(128)}, f32[2,256]{1,0:T(2,128)S(1)}) all-reduce(f32[2,256]{1,0:T(2,128)S(1)} %get-tuple-element.4, f32[]{:T(128)S(6)} %convert_element_type.49, f32[2,256]{1,0:T(2,128)S(1)} %get-tuple-element.3), channel_id=1, replica_groups=mesh['nodes_0'=4,'nodes_1'=8,'nodes_2'=4,'feat'=2] {'nodes_0'}, use_global_device_ids=true, to_apply=%region_3.4 | all-reduce | flops 1025 | bytes 8200 | tf_op jit(solution)/shard_map/psum | solution.py:30
  468.7 16.1 %all-reduce.1 = (f32[2,256]{1,0:T(2,128)S(1)}, f32[]{:T(128)}, f32[2,256]{1,0:T(2,128)S(1)}) all-reduce(f32[2,256]{1,0:T(2,128)S(1)} %get-tuple-element.15, f32[]{:T(128)} %get-tuple-element.16, f32[2,256]{1,0:T(2,128)S(1)} %get-tuple-element.17), channel_id=1, replica_groups=mesh['nodes_0'=4,'nodes_1'=8,'nodes_2'=4,'feat'=2] {'nodes_1'}, use_global_device_ids=true, to_apply=%region_4.5 | all-reduce | flops 1025 | bytes 8200 | tf_op jit(solution)/shard_map/psum | solution.py:30
  484.7 9.1 %all-reduce.2 = (f32[2,256]{1,0:T(2,128)S(1)}, f32[]{:T(128)}, f32[2,256]{1,0:T(2,128)S(1)}) all-reduce(f32[2,256]{1,0:T(2,128)S(1)} %get-tuple-element.9, f32[]{:T(128)} %get-tuple-element.10, f32[2,256]{1,0:T(2,128)S(1)} %get-tuple-element.11), channel_id=1, replica_groups=mesh['nodes_0'=4,'nodes_1'=8,'nodes_2'=4,'feat'=2] {'nodes_2'}, use_global_device_ids=true, to_apply=%region_5.6 | all-reduce | flops 1025 | bytes 8200 | tf_op jit(solution)/shard_map/psum | solution.py:30
  493.8 0.7 add_sqrt_fusion
  494.5 0.2 multiply_convert_fusion
  494.6 0.0 copy-start.4
  494.7 0.0 copy-start.11
  494.7 0.0 copy-start.1
  494.7 0.1 copy.25
  494.9 12.1 %all_to_all.21 = bf16[2,512,256]{1,2,0:T(8,128)(2,1)S(1)} all-to-all(bf16[2,512,256]{1,2,0:T(8,128)(2,1)S(1)} %broadcast_in_dim.8), channel_id=1, replica_groups=mesh['nodes_0'=4,'nodes_1'=8,'nodes_2'=4,'feat'=2] {'feat'}, dimensions={0} | all-to-all | bytes 1048576 | tf_op jit(solution)/shard_map/all_to_all | solution.py:19
  507.0 1.1 fusion.32
  508.1 0.0 reduce-scatter.3.cloned.1.call-update
  508.1 0.0 reduce-scatter.5.cloned.1.call-start
  508.2 16.2 %reduce-scatter.3.cloned.1.call-done = f32[128,256]{1,0:T(8,128)} async-done(((f32[512,256]{1,0:T(8,128)}), f32[128,256]{1,0:T(8,128)}) %reduce-scatter.3.cloned.1.call-update) | async-done | bytes 131088 | tf_op jit(solution)/shard_map/reduce_scatter | solution.py:36
  524.4 0.0 reduce-scatter.5.cloned.1.call-update
  524.4 0.6 dynamic-slice
  525.7 34.7 %reduce-scatter.5.cloned.1.call-done = f32[16,256]{1,0:T(8,128)} async-done(((f32[128,256]{1,0:T(8,128)}), f32[16,256]{1,0:T(8,128)}) %reduce-scatter.5.cloned.1.call-update) | async-done | bytes 16400 | tf_op jit(solution)/shard_map/reduce_scatter | solution.py:36
  560.5 13.7 %all-reduce = f32[16,256]{1,0:T(8,128)S(1)} all-reduce(f32[16,256]{1,0:T(8,128)} %reduce-scatter.5.cloned.1.call-done), channel_id=4, replica_groups=mesh['nodes_0'=4,'nodes_1'=8,'nodes_2'=4,'feat'=2] {'nodes_2'}, use_global_device_ids=true, to_apply=%region_15.16.clone | all-reduce | flops 4096 | bytes 32768
  574.2 1.9 select_reduce_fusion.2
  576.1 9.0 %psum.100 = f32[]{:T(128)} all-reduce(f32[]{:T(128)} %get-tuple-element.18), channel_id=1, replica_groups=mesh['nodes_0'=4,'nodes_1'=8,'nodes_2'=4,'feat'=2] {'nodes_0'}, use_global_device_ids=true, to_apply=%region_17.18 | all-reduce | flops 1 | bytes 8 | tf_op jit(solution)/shard_map/psum | solution.py:30
  585.1 12.6 %psum.101 = f32[]{:T(128)} all-reduce(f32[]{:T(128)} %psum.100), channel_id=1, replica_groups=mesh['nodes_0'=4,'nodes_1'=8,'nodes_2'=4,'feat'=2] {'nodes_1'}, use_global_device_ids=true, to_apply=%region_18.19 | all-reduce | flops 1 | bytes 8 | tf_op jit(solution)/shard_map/psum | solution.py:30
  597.7 6.6 %psum.102 = f32[]{:T(128)} all-reduce(f32[]{:T(128)} %psum.101), channel_id=1, replica_groups=mesh['nodes_0'=4,'nodes_1'=8,'nodes_2'=4,'feat'=2] {'nodes_2'}, use_global_device_ids=true, to_apply=%region_19.20 | all-reduce | flops 1 | bytes 8 | tf_op jit(solution)/shard_map/psum | solution.py:30
  604.3 19.9 %psum.103 = f32[]{:T(128)} all-reduce(f32[]{:T(128)} %psum.102), channel_id=1, replica_groups=mesh['nodes_0'=4,'nodes_1'=8,'nodes_2'=4,'feat'=2] {'feat'}, use_global_device_ids=true, to_apply=%region_20.21 | all-reduce | flops 1 | bytes 8 | tf_op jit(solution)/shard_map/psum | solution.py:30
  (35 shorter events, 0.3 us)
Async XLA Ops:
  7.2 143.4 %copy-start = (bf16[512,256]{1,0:T(8,128)(2,1)S(1)}, bf16[512,256]{1,0:T(8,128)(2,1)}, u32[]{:S(2)}) copy-start(bf16[512,256]{1,0:T(8,128)(2,1)} %param.17) | copy-start | bytes 786436
  7.2 1.0 copy-start.2
  37.5 16.5 %copy-start.6 = (s32[2,4096]{1,0:T(2,128)S(1)}, s32[2,4096]{1,0:T(2,128)}, u32[]{:S(2)}) copy-start(s32[2,4096]{1,0:T(2,128)} %param.13) | copy-start | bytes 98308
  37.5 16.6 %copy-start.7 = (s32[2,4096]{1,0:T(2,128)S(1)}, s32[2,4096]{1,0:T(2,128)}, u32[]{:S(2)}) copy-start(s32[2,4096]{1,0:T(2,128)} %param.14) | copy-start | bytes 98308
  37.5 17.4 %copy-start.8 = (s32[2,4096]{1,0:T(2,128)S(1)}, s32[2,4096]{1,0:T(2,128)}, u32[]{:S(2)}) copy-start(s32[2,4096]{1,0:T(2,128)} %param.12) | copy-start | bytes 98308
  37.5 65.8 %all-to-all-start = ((bf16[128,64,128]{2,1,0:T(8,128)(2,1)}), bf16[128,64,128]{2,1,0:T(8,128)(2,1)S(1)}, u32[]{:S(2)}, u32[]{:S(2)}) async-start(bf16[128,64,128]{2,1,0:T(8,128)(2,1)} %bitcast.1), calls=%async_computation | async-start | bytes 4194304 | tf_op jit(solution)/shard_map/all_to_all | solution.py:80
  103.3 1.4 copy-start.3
  138.7 2.5 copy-start.9
  138.8 2.5 copy-start.10
  224.0 188.5 %all-to-all-start.2 = ((bf16[2,128,64,256]{3,2,0,1:T(8,128)(2,1)}), bf16[2,128,64,256]{3,2,0,1:T(8,128)(2,1)}, u32[]{:S(2)}, u32[]{:S(2)}) async-start(bf16[2,128,64,256]{3,2,0,1:T(8,128)(2,1)} %bitcast.75), calls=%async_computation.2 | async-start | bytes 16777216 | tf_op jit(solution)/shard_map/all_to_all | solution.py:95
  231.7 292.7 %reduce-scatter.3.cloned.1.call-start = ((), (), s32[]{:S(2)}) async-start(), calls=%async_computation.6 | async-start | bytes 655360 | tf_op jit(solution)/shard_map/reduce_scatter | solution.py:36
  458.4 1.3 copy-start.5
  494.6 13.5 %copy-start.4 = (bf16[2,512,256]{2,1,0:T(8,128)(2,1)}, bf16[2,512,256]{2,1,0:T(8,128)(2,1)S(1)}, u32[]{:S(2)}) copy-start(bf16[2,512,256]{2,1,0:T(8,128)(2,1)S(1)} %multiply_convert_fusion) | copy-start | bytes 1572868
  494.7 29.8 %copy-start.11 = (u32[256]{0:T(256)S(1)}, u32[256]{0:T(256)}, u32[]{:S(2)}) copy-start(u32[256]{0:T(256)} %constant.49) | copy-start | bytes 3076
  494.7 129.6 %copy-start.1 = (bf16[512,256]{1,0:T(8,128)(2,1)S(1)}, bf16[512,256]{1,0:T(8,128)(2,1)}, u32[]{:S(2)}) copy-start(bf16[512,256]{1,0:T(8,128)(2,1)} %param.17) | copy-start | bytes 786436
  508.1 52.3 %reduce-scatter.5.cloned.1.call-start = ((), (), s32[]{:S(2)}) async-start(), calls=%async_computation.7 | async-start | bytes 147456 | tf_op jit(solution)/shard_map/reduce_scatter | solution.py:36
Sparse Core Ops, SparseCore 0:
  508.3 16.0 reduce-scatter.2
  526.9 33.5 reduce-scatter.4
where the time goes:
time: 632 us; the launch traced here: 631 us
  waiting for transfers between devices  279 us (44%)
  local copies, waits for them, and re-layouts  172 us (27%)
  blocking collectives  116 us (18%)
  starting transfers between devices  24.2 us (4%)
  between operations  15.8 us (2%)
  other arithmetic  13.5 us (2%)
  matrix products  10.7 us (2%)
    all_to_all x1, waiting for transfers between devices, per_device(): lax.all_to_all(projected[:, outbound], NODES, split_axis=1, concat_axis=1...  180 us
    psum x7, blocking collectives, over_axes(): shard = lax.psum(shard, axis)  81.8 us
    gather x2, local copies, waits for them, and re-layouts, per_device(): projected[:, outbound]  72.5 us
    gather x4, local copies, waits for them, and re-layouts, mix_view(): lookup[edge_src[view_index]].astype(jnp.float32)  61.4 us
    reduce_scatter x2, waiting for transfers between devices, own_rows(): running = lax.psum_scatter(running, axis, scatter_dimension=0, tiled=True)  51 us
    all_to_all x1, waiting for transfers between devices, per_device(): lax.all_to_all(features[outbound], NODES, split_axis=0, concat_axis=0, ti...  48.3 us
    gather x1, local copies, waits for them, and re-layouts, per_device(): features[outbound]  29.2 us
    all_to_all x2, blocking collectives, from_everyone(): lax.all_to_all(jnp.broadcast_to(shard[None], (devices, *shard.shape)), ax...  20.3 us
  transfers between devices with their start and end apart: 4, of which 4 were waited for; matrix products, arithmetic and copies ran while one was open for 0% of the time, Pallas kernels for 0%

commit v1 on v0

--- a/solution.py
+++ b/solution.py
@@ -27,7 +27,8 @@
 
 def over_axes(shard, axes):
     for axis in axes:
-        shard = lax.psum(shard, axis)
+        parts = lax.all_gather(shard, axis)
+        shard = jnp.sum(parts, axis=0)
     return shard
 
 

time: 632 us -> 711 us (1.12)
  blocking collectives: 116 us -> 356 us
  waiting for transfers between devices: 279 us -> 103 us
  local copies, waits for them, and re-layouts: 172 us -> 183 us
    unnamed x1 -> x8, blocking collectives: 13.7 us -> 252 us
    all_to_all x1, waiting for transfers between devices: 180 us -> 0.01 us  [per_device(): lax.all_to_all(projected[:, outbound], NODES, split_axis=1, concat_axis=1...]
    psum x7 -> x0, blocking collectives: 81.8 us -> none  [over_axes(): shard = lax.psum(shard, axis)]
    all_gather x0 -> x6, blocking collectives: none -> 64.7 us  [over_axes(): parts = lax.all_gather(shard, axis)]
    all_to_all x2, blocking collectives: 20.3 us -> 39.7 us  [from_everyone(): lax.all_to_all(jnp.broadcast_to(shard[None], (devices, *shard.shape)), ax...]
    unnamed x25 -> x48, local copies, waits for them, and re-layouts: 2 us -> 13 us
  transfers between devices with their start and end apart: 4 -> 4, of which waited for: 4 -> 3; matrix products, arithmetic and copies ran while one was open for 0% -> 1% of each run, Pallas kernels for 0% -> 0%
where the time goes in v1:
time: 711 us; the launch traced here: 710 us
  blocking collectives  356 us (50%)
  local copies, waits for them, and re-layouts  183 us (26%)
  waiting for transfers between devices  103 us (14%)
  starting transfers between devices  24.3 us (3%)
  other arithmetic  17.7 us (2%)
  between operations  15.8 us (2%)
  matrix products  10.7 us (2%)
    unnamed x8, blocking collectives  252 us
    gather x2, local copies, waits for them, and re-layouts, per_device(): projected[:, outbound]  72.5 us
    all_gather x6, blocking collectives, over_axes(): parts = lax.all_gather(shard, axis)  64.7 us
    gather x4, local copies, waits for them, and re-layouts, mix_view(): lookup[edge_src[view_index]].astype(jnp.float32)  61.4 us
    reduce_scatter x2, waiting for transfers between devices, own_rows(): running = lax.psum_scatter(running, axis, scatter_dimension=0, tiled=True)  54.4 us
    all_to_all x1, waiting for transfers between devices, per_device(): lax.all_to_all(features[outbound], NODES, split_axis=0, concat_axis=0, ti...  48.3 us
    all_to_all x2, blocking collectives, from_everyone(): lax.all_to_all(jnp.broadcast_to(shard[None], (devices, *shard.shape)), ax...  39.7 us
    gather x1, local copies, waits for them, and re-layouts, per_device(): features[outbound]  29.2 us
  transfers between devices with their start and end apart: 4, of which 3 were waited for; matrix products, arithmetic and copies ran while one was open for 1% of the time, Pallas kernels for 0%

profile of v1, /device:TPU:1, one launch (start us, length us, event | category | flops | bytes accessed | tf_op | source)
XLA Modules:
  0.0 710.0 jit_solution(10667455482702117308)
XLA Ops:
  7.2 0.8 compare_select_fusion.2
  8.2 29.2 %gather_fusion = bf16[8192,128]{1,0:T(8,128)(2,1)} fusion(bf16[512,128]{1,0:T(8,128)(2,1)S(1)} %copy-done.2, s32[8192]{0:T(1024)S(1)} %broadcast_clamp_fusion), kind=kCustom, calls=%fused_computation | custom fusion | bytes 4227072 | tf_op jit(solution)/shard_map/gather | solution.py:81
  37.5 16.5 %all-to-all-start = ((bf16[128,64,128]{2,1,0:T(8,128)(2,1)}), bf16[128,64,128]{2,1,0:T(8,128)(2,1)S(1)}, u32[]{:S(2)}, u32[]{:S(2)}) async-start(bf16[128,64,128]{2,1,0:T(8,128)(2,1)} %bitcast.1), calls=%async_computation | async-start | bytes 4194304 | tf_op jit(solution)/shard_map/all_to_all | solution.py:81
  54.3 0.5 select_reduce_fusion
  55.0 48.3 %all-to-all-done = bf16[128,64,128]{2,1,0:T(8,128)(2,1)S(1)} async-done(((bf16[128,64,128]{2,1,0:T(8,128)(2,1)}), bf16[128,64,128]{2,1,0:T(8,128)(2,1)S(1)}, u32[]{:S(2)}, u32[]{:S(2)}) %all-to-all-start) | async-done | bytes 2097184 | tf_op jit(solution)/shard_map/all_to_all | solution.py:81
  103.3 1.3 copy-done.3
  104.6 1.8 pad_maximum_fusion.2
  106.5 14.9 %gather_fusion.1 = bf16[4096,128]{1,0:T(8,128)(2,1)} fusion(bf16[8704,128]{1,0:T(8,128)(2,1)S(1)} %pad_maximum_fusion.2, s32[4096]{0:T(1024)S(1)} %broadcast_clamp_fusion.2), kind=kCustom, calls=%fused_computation.1 | custom fusion | bytes 2113536 | tf_op jit(solution)/shard_map/gather | solution.py:68
  121.4 2.5 fusion.6
  123.9 14.9 %gather_fusion.2 = bf16[4096,128]{1,0:T(8,128)(2,1)} fusion(bf16[8704,128]{1,0:T(8,128)(2,1)S(1)} %pad_maximum_fusion.2, s32[4096]{0:T(1024)S(1)} %broadcast_clamp_fusion.1), kind=kCustom, calls=%fused_computation.2 | custom fusion | bytes 2113536 | tf_op jit(solution)/shard_map/gather | solution.py:68
  138.8 2.5 fusion.2
  141.3 0.4 fusion.13
  141.7 0.4 fusion.12
  142.3 8.2 %all_to_all.20 = bf16[2,2,512,256]{3,2,1,0:T(8,128)(2,1)S(1)} all-to-all(bf16[2,2,512,256]{3,2,1,0:T(8,128)(2,1)S(1)} %broadcast_in_dim.6), channel_id=1, replica_groups=mesh['nodes_0'=4,'nodes_1'=8,'nodes_2'=4,'feat'=2] {'feat'}, dimensions={0} | all-to-all | bytes 2097152 | tf_op jit(solution)/shard_map/all_to_all | solution.py:19
  150.6 0.4 convolution_convert_fusion
  151.0 0.5 copy.21
  151.6 63.9 %gather_fusion.3 = bf16[8192,2,256]{2,1,0:T(2,128)(2,1)} fusion(bf16[2,512,256]{2,0,1:T(2,128)(2,1)S(1)} %copy.21, s32[8192]{0:T(1024)S(1)} %broadcast_clamp_fusion), kind=kCustom, calls=%fused_computation.3 | custom fusion | bytes 16809984 | tf_op jit(solution)/shard_map/gather | solution.py:97
  215.5 8.6 %copy.30 = bf16[128,64,2,256]{3,1,2,0:T(8,128)(2,1)} copy(bf16[128,64,2,256]{3,2,1,0:T(2,128)(2,1)} %bitcast.93) | data formatting | bytes 16777216 | tf_op jit(solution)/shard_map/gather | solution.py:97
  224.0 7.8 %all-to-all-start.2 = ((bf16[2,128,64,256]{3,2,0,1:T(8,128)(2,1)}), bf16[2,128,64,256]{3,2,0,1:T(8,128)(2,1)}, u32[]{:S(2)}, u32[]{:S(2)}) async-start(bf16[2,128,64,256]{3,2,0,1:T(8,128)(2,1)} %bitcast.92), calls=%async_computation.2 | async-start | bytes 16777216 | tf_op jit(solution)/shard_map/all_to_all | solution.py:96
  232.5 0.6 dynamic-slice
  233.1 0.7 dynamic-update-slice
  233.8 13.6 %all-reduce = f32[4]{0:T(128)S(1)} all-reduce(f32[4]{0:T(128)S(1)} %dynamic-update-slice), channel_id=1, replica_groups=mesh['nodes_0'=4,'nodes_1'=8,'nodes_2'=4,'feat'=2] {'nodes_0'}, use_global_device_ids=true, to_apply=%add | all-reduce | flops 4 | bytes 32
  247.4 0.7 dynamic-slice.1
  248.0 0.6 reduce_sum.168
  248.6 1.4 dynamic-update-slice.1
  250.1 170.6 %all-reduce.1 = f32[8]{0:T(128)S(1)} all-reduce(f32[8]{0:T(128)S(1)} %dynamic-update-slice.1), channel_id=1, replica_groups=mesh['nodes_0'=4,'nodes_1'=8,'nodes_2'=4,'feat'=2] {'nodes_1'}, use_global_device_ids=true, to_apply=%add.1 | all-reduce | flops 8 | bytes 64
  420.7 0.6 reduce_sum.169
  421.3 0.6 fusion.42
  421.9 1.4 dynamic-update-slice.2
  423.3 8.0 %all-reduce.2 = f32[4]{0:T(128)S(1)} all-reduce(f32[4]{0:T(128)S(1)} %dynamic-update-slice.2), channel_id=1, replica_groups=mesh['nodes_0'=4,'nodes_1'=8,'nodes_2'=4,'feat'=2] {'nodes_2'}, use_global_device_ids=true, to_apply=%add.2 | all-reduce | flops 4 | bytes 32
  431.3 0.6 reduce_sum.170
  432.0 5.3 fusion.41
  437.3 2.8 pad_maximum_fusion.1
  440.1 15.8 %gather_fusion.5 = bf16[4096,256]{1,0:T(8,128)(2,1)S(1)} fusion(bf16[8704,256]{1,0:T(8,128)(2,1)} %pad_maximum_fusion.1, s32[4096]{0:T(1024)S(1)} %broadcast_clamp_fusion.1), kind=kCustom, calls=%fused_computation.5 | custom fusion | bytes 4210688 | tf_op jit(solution)/shard_map/gather | solution.py:68
  456.0 2.1 fusion
  458.0 4.0 pad_maximum_fusion
  462.1 15.8 %gather_fusion.4 = bf16[4096,256]{1,0:T(8,128)(2,1)S(1)} fusion(bf16[8704,256]{1,0:T(8,128)(2,1)} %pad_maximum_fusion, s32[4096]{0:T(1024)S(1)} %broadcast_clamp_fusion.2), kind=kCustom, calls=%fused_computation.4 | custom fusion | bytes 4210688 | tf_op jit(solution)/shard_map/gather | solution.py:68
  477.9 1.3 fusion.4
  479.7 8.7 %all-gather.6 = f32[4,2,256]{2,1,0:T(2,128)S(1)} all-gather(f32[1,2,256]{2,1,0:T(2,128)S(1)} %bitcast.109), channel_id=2, replica_groups=mesh['nodes_0'=4,'nodes_1'=8,'nodes_2'=4,'feat'=2] {'nodes_0'}, dimensions={0}, use_global_device_ids=true | all-gather | bytes 10240 | tf_op jit(solution)/shard_map/all_gather | solution.py:30
  488.4 16.0 %all-gather.7 = f32[8,2,256]{2,1,0:T(2,128)S(1)} all-gather(f32[1,2,256]{2,1,0:T(2,128)S(1)} %bitcast.112), channel_id=3, replica_groups=mesh['nodes_0'=4,'nodes_1'=8,'nodes_2'=4,'feat'=2] {'nodes_1'}, dimensions={0}, use_global_device_ids=true | all-gather | bytes 18432 | tf_op jit(solution)/shard_map/all_gather | solution.py:30
  504.4 8.1 %all-gather.8 = f32[4,2,256]{2,1,0:T(2,128)S(1)} all-gather(f32[1,2,256]{2,1,0:T(2,128)S(1)} %bitcast.110), channel_id=4, replica_groups=mesh['nodes_0'=4,'nodes_1'=8,'nodes_2'=4,'feat'=2] {'nodes_2'}, dimensions={0}, use_global_device_ids=true | all-gather | bytes 10240 | tf_op jit(solution)/shard_map/all_gather | solution.py:30
  512.5 8.1 %all-gather.9 = f32[4,2,256]{2,1,0:T(2,128)S(1)} all-gather(f32[1,2,256]{2,1,0:T(2,128)S(1)} %bitcast.108), channel_id=5, replica_groups=mesh['nodes_0'=4,'nodes_1'=8,'nodes_2'=4,'feat'=2] {'nodes_0'}, dimensions={0}, use_global_device_ids=true | all-gather | bytes 10240 | tf_op jit(solution)/shard_map/all_gather | solution.py:30
  520.7 15.6 %all-gather.10 = f32[8,2,256]{2,1,0:T(2,128)S(1)} all-gather(f32[1,2,256]{2,1,0:T(2,128)S(1)} %bitcast.113), channel_id=6, replica_groups=mesh['nodes_0'=4,'nodes_1'=8,'nodes_2'=4,'feat'=2] {'nodes_1'}, dimensions={0}, use_global_device_ids=true | all-gather | bytes 18432 | tf_op jit(solution)/shard_map/all_gather | solution.py:30
  536.3 8.1 %all-gather.11 = f32[4,2,256]{2,1,0:T(2,128)S(1)} all-gather(f32[1,2,256]{2,1,0:T(2,128)S(1)} %bitcast.111), channel_id=7, replica_groups=mesh['nodes_0'=4,'nodes_1'=8,'nodes_2'=4,'feat'=2] {'nodes_2'}, dimensions={0}, use_global_device_ids=true | all-gather | bytes 10240 | tf_op jit(solution)/shard_map/all_gather | solution.py:30
  544.4 0.6 add_sqrt_fusion
  545.5 31.5 %all_to_all.21 = bf16[2,512,256]{1,2,0:T(8,128)(2,1)S(1)} all-to-all(bf16[2,512,256]{1,2,0:T(8,128)(2,1)S(1)} %broadcast_in_dim.8), channel_id=1, replica_groups=mesh['nodes_0'=4,'nodes_1'=8,'nodes_2'=4,'feat'=2] {'feat'}, dimensions={0} | all-to-all | bytes 1048576 | tf_op jit(solution)/shard_map/all_to_all | solution.py:19
  577.0 1.1 fusion.32
  578.2 19.0 %reduce-scatter.3.cloned.1.call-done = f32[128,256]{1,0:T(8,128)} async-done(((f32[512,256]{1,0:T(8,128)}), f32[128,256]{1,0:T(8,128)}) %reduce-scatter.3.cloned.1.call-update) | async-done | bytes 131088 | tf_op jit(solution)/shard_map/reduce_scatter | solution.py:37
  597.9 35.4 %reduce-scatter.5.cloned.1.call-done = f32[16,256]{1,0:T(8,128)} async-done(((f32[128,256]{1,0:T(8,128)}), f32[16,256]{1,0:T(8,128)}) %reduce-scatter.5.cloned.1.call-update) | async-done | bytes 16400 | tf_op jit(solution)/shard_map/reduce_scatter | solution.py:37
  633.3 13.6 %all-reduce.7 = f32[16,256]{1,0:T(8,128)S(1)} all-reduce(f32[16,256]{1,0:T(8,128)} %reduce-scatter.5.cloned.1.call-done), channel_id=10, replica_groups=mesh['nodes_0'=4,'nodes_1'=8,'nodes_2'=4,'feat'=2] {'nodes_2'}, use_global_device_ids=true, to_apply=%region_15.16.clone | all-reduce | flops 4096 | bytes 32768
  646.9 1.8 select_reduce_fusion.2
  648.8 1.3 dynamic-update-slice.3
  650.1 8.4 %all-reduce.3 = f32[4]{0:T(128)S(1)} all-reduce(f32[4]{0:T(128)S(1)} %dynamic-update-slice.3), channel_id=1, replica_groups=mesh['nodes_0'=4,'nodes_1'=8,'nodes_2'=4,'feat'=2] {'nodes_0'}, use_global_device_ids=true, to_apply=%add.3 | all-reduce | flops 4 | bytes 32
  658.5 0.6 reduce_sum.176
  659.1 1.4 dynamic-update-slice.4
  660.6 12.0 %all-reduce.4 = f32[8]{0:T(128)S(1)} all-reduce(f32[8]{0:T(128)S(1)} %dynamic-update-slice.4), channel_id=1, replica_groups=mesh['nodes_0'=4,'nodes_1'=8,'nodes_2'=4,'feat'=2] {'nodes_1'}, use_global_device_ids=true, to_apply=%add.4 | all-reduce | flops 8 | bytes 64
  672.6 0.6 reduce_sum.177
  673.2 1.4 dynamic-update-slice.5
  674.5 0.7 dynamic-slice.6
  675.2 6.1 all-reduce.5
  681.2 0.6 reduce_sum.178
  681.9 1.4 dynamic-update-slice.6
  683.3 19.3 %all-reduce.6 = f32[2]{0:T(128)S(1)} all-reduce(f32[2]{0:T(128)S(1)} %dynamic-update-slice.6), channel_id=1, replica_groups=mesh['nodes_0'=4,'nodes_1'=8,'nodes_2'=4,'feat'=2] {'feat'}, use_global_device_ids=true, to_apply=%add.6 | all-reduce | flops 2 | bytes 16
  702.6 0.6 reduce_sum.179
  (77 shorter events, 1.9 us)
Async XLA Ops:
  7.2 143.4 %copy-start = (bf16[512,256]{1,0:T(8,128)(2,1)S(1)}, bf16[512,256]{1,0:T(8,128)(2,1)}, u32[]{:S(2)}) copy-start(bf16[512,256]{1,0:T(8,128)(2,1)} %param.17) | copy-start | bytes 786436
  7.2 1.0 copy-start.2
  37.5 16.5 %copy-start.6 = (s32[2,4096]{1,0:T(2,128)S(1)}, s32[2,4096]{1,0:T(2,128)}, u32[]{:S(2)}) copy-start(s32[2,4096]{1,0:T(2,128)} %param.13) | copy-start | bytes 98308
  37.5 16.6 %copy-start.7 = (s32[2,4096]{1,0:T(2,128)S(1)}, s32[2,4096]{1,0:T(2,128)}, u32[]{:S(2)}) copy-start(s32[2,4096]{1,0:T(2,128)} %param.14) | copy-start | bytes 98308
  37.5 17.4 %copy-start.8 = (s32[2,4096]{1,0:T(2,128)S(1)}, s32[2,4096]{1,0:T(2,128)}, u32[]{:S(2)}) copy-start(s32[2,4096]{1,0:T(2,128)} %param.12) | copy-start | bytes 98308
  37.5 65.8 %all-to-all-start = ((bf16[128,64,128]{2,1,0:T(8,128)(2,1)}), bf16[128,64,128]{2,1,0:T(8,128)(2,1)S(1)}, u32[]{:S(2)}, u32[]{:S(2)}) async-start(bf16[128,64,128]{2,1,0:T(8,128)(2,1)} %bitcast.1), calls=%async_computation | async-start | bytes 4194304 | tf_op jit(solution)/shard_map/all_to_all | solution.py:81
  103.3 1.4 copy-start.3
  138.7 2.5 copy-start.10
  138.8 2.5 copy-start.11
  224.0 8.5 %copy-start.14 = (u32[256]{0:T(256)S(1)}, u32[256]{0:T(256)}, u32[]{:S(2)}) copy-start(u32[256]{0:T(256)} %constant.49) | copy-start | bytes 3076
  224.0 23.4 %copy-start.13 = (u32[256]{0:T(256)S(1)}, u32[256]{0:T(256)}, u32[]{:S(2)}) copy-start(u32[256]{0:T(256)} %constant.54) | copy-start | bytes 3076
  224.0 197.3 %copy-start.9 = (u32[256]{0:T(256)S(1)}, u32[256]{0:T(256)}, u32[]{:S(2)}) copy-start(u32[256]{0:T(256)} %constant.59) | copy-start | bytes 3076
  224.0 207.9 %all-to-all-start.2 = ((bf16[2,128,64,256]{3,2,0,1:T(8,128)(2,1)}), bf16[2,128,64,256]{3,2,0,1:T(8,128)(2,1)}, u32[]{:S(2)}, u32[]{:S(2)}) async-start(bf16[2,128,64,256]{3,2,0,1:T(8,128)(2,1)} %bitcast.92), calls=%async_computation.2 | async-start | bytes 16777216 | tf_op jit(solution)/shard_map/all_to_all | solution.py:96
  231.8 365.3 %reduce-scatter.3.cloned.1.call-start = ((), (), s32[]{:S(2)}) async-start(), calls=%async_computation.6 | async-start | bytes 655360 | tf_op jit(solution)/shard_map/reduce_scatter | solution.py:37
  477.9 1.3 copy-start.5
  545.3 32.9 %copy-start.4 = (bf16[2,512,256]{2,1,0:T(8,128)(2,1)}, bf16[2,512,256]{2,1,0:T(8,128)(2,1)S(1)}, u32[]{:S(2)}) copy-start(bf16[2,512,256]{2,1,0:T(8,128)(2,1)S(1)} %multiply_convert_fusion) | copy-start | bytes 1572868
  545.3 129.2 %copy-start.12 = (u32[256]{0:T(256)S(1)}, u32[256]{0:T(256)}, u32[]{:S(2)}) copy-start(u32[256]{0:T(256)} %constant.79) | copy-start | bytes 3076
  545.3 157.9 %copy-start.1 = (bf16[512,256]{1,0:T(8,128)(2,1)S(1)}, bf16[512,256]{1,0:T(8,128)(2,1)}, u32[]{:S(2)}) copy-start(bf16[512,256]{1,0:T(8,128)(2,1)} %param.17) | copy-start | bytes 786436
  578.1 55.1 %reduce-scatter.5.cloned.1.call-start = ((), (), s32[]{:S(2)}) async-start(), calls=%async_computation.7 | async-start | bytes 147456 | tf_op jit(solution)/shard_map/reduce_scatter | solution.py:37
Sparse Core Ops, SparseCore 0:
  578.3 18.8 reduce-scatter.2
  599.7 33.5 reduce-scatter.4
